TPU v7x, 32 devices: a whole 2x2x4 slice. The times are simulated.
32 devices in a mesh: grp: 2 (over y), seq: 4 (over z), head: 2 (over x), rep: 2 (over core).
Axes of the slice: x: 2, y: 2, z: 4, core: 2. Of those that a mesh axis runs over, the one named last changes fastest.
Arguments:
- queries: bfloat16 [32, 64, 128], P(('grp', 'rep'), 'head'), parts along dimension 0, may hold values from -16 to 16
- key_cache: bfloat16 [32, 4, 2048, 128], P(('grp', 'rep'), 'head', 'seq'), parts along dimension 0, may hold values from -7 to 7
- value_cache: bfloat16 [32, 4, 2048, 128], P(('grp', 'rep'), 'head', 'seq'), parts along dimension 0, may hold values from -6 to 6
- indices: int32 [32, 4, 16], P(('grp', 'rep'), 'head'), parts along dimension 0, may hold values from 0 to 31, as said below
- counts: int32 [32, 4], P(('grp', 'rep'), 'head'), parts along dimension 0, may hold values from 8 to 16, as said below
- lengths: int32 [32], P(('grp', 'rep')), parts along dimension 0, may hold values from 1024 to 2048
Outputs:
- attended: bfloat16 [32, 64, 128], P(('grp', 'rep'), 'head', 'seq'), parts along dimension 0
There are 2 independent parts, one for each index of `grp`. A program takes and returns all parts, laid end to end along the dimension named above; each array names one. Nothing has to cross between parts.
Inputs may be any that keep to these rules, and one draw needn't show every extreme that they name: `indices`: within a row and key-value head the 16 blocks are distinct, and each holds at least one token below the row's length. `counts`: some row uses all 16 slots.
All inputs are finite; a program needn't handle non-finite values.
Results may differ from a plain program's by a relative error of at most 0.0015.
Values sent between devices are 32-bit elements; how exact they have to be, the bound alone decides.
A program may use at most 64 MiB of HBM per device.

v0:
```python
import jax
import jax.numpy as jnp
from jax import lax
from jax.sharding import PartitionSpec as P

BLOCK = 64
SLOTS = 16


lowest = -1e30


def joined(value, axis, join):
    pieces = jax.tree.map(lambda part: lax.all_gather(part, axis), value)
    head = jax.tree.map(lambda part: part[0], pieces)
    tail = jax.tree.map(lambda part: part[1:], pieces)
    subtotal, _ = lax.scan(lambda subtotal, section: (join(subtotal, section), None), head, tail)
    return subtotal


def join_partials(first, second):
    first_running_max, first_total, first_summed = first
    second_running_max, second_total, second_summed = second
    highest = jnp.maximum(first_running_max, second_running_max)
    first_factor = jnp.exp(first_running_max - highest)
    second_factor = jnp.exp(second_running_max - highest)
    total = first_total * first_factor + second_total * second_factor
    weighted_value_sum = (
        first_summed * first_factor[..., None] + second_summed * second_factor[..., None]
    )
    return (highest, total, weighted_value_sum)


def local(queries, key_cache, value_cache, indices, counts, lengths):
    batch_rows, heads_local, ctx_local, key_width = key_cache.shape
    value_width = value_cache.shape[3]
    group = queries.shape[1] // heads_local
    rescale_factor = key_width ** (-0.5)
    seq_index = lax.axis_index("seq")
    seq_count = lax.axis_size("seq")
    query_grouped = queries.reshape(batch_rows, heads_local, group, key_width)
    slot_used = jnp.arange(SLOTS, dtype=jnp.int32)[None, None, :] < counts[:, :, None]
    position = seq_index * ctx_local + jnp.arange(ctx_local, dtype=jnp.int32)
    block_number = position // BLOCK
    matches = (indices[:, :, :, None] == block_number[None, None, None, :]) & slot_used[
        :, :, :, None
    ]
    picked = jnp.any(matches, axis=2)
    live = picked & (position[None, None, :] < lengths[:, None, None])
    scores = (
        jnp.einsum("bhgd,bhkd->bhgk", query_grouped, key_cache, preferred_element_type=jnp.float32)
        * rescale_factor
    )
    scores = jnp.where(live[:, :, None, :], scores, -jnp.inf)
    local_top = jnp.maximum(jnp.max(scores, axis=-1), lowest)
    softmax_weights = jnp.exp(scores - local_top[..., None])
    local_total = jnp.sum(softmax_weights, axis=-1)
    local_summed = jnp.einsum(
        "bhgk,bhkv->bhgv",
        softmax_weights,
        value_cache.astype(jnp.float32),
        precision=lax.Precision.HIGHEST,
    )
    share_width = value_width // seq_count
    highest, total, weighted_value_sum = joined(
        (local_top, local_total, local_summed), "seq", join_partials
    )
    result = (weighted_value_sum / total[..., None]).reshape(
        batch_rows, heads_local * group, value_width
    )
    result = lax.dynamic_slice_in_dim(result, seq_index * share_width, share_width, 2)
    return result.astype(jnp.bfloat16)


def solution(mesh):
    return jax.shard_map(
        local,
        mesh=mesh,
        in_specs=(
            P(("grp", "rep"), "head", None),
            P(("grp", "rep"), "head", "seq", None),
            P(("grp", "rep"), "head", "seq", None),
            P(("grp", "rep"), "head", None),
            P(("grp", "rep"), "head"),
            P(("grp", "rep")),
        ),
        out_specs=P(("grp", "rep"), "head", "seq"),
        check_vma=False,
    )
```

profile of v0, /device:TPU:0, one launch (start us, length us, event | category | flops | bytes accessed | tf_op | source)
XLA Modules:
  0.0 50.9 jit_solution(10579788579333582362)
XLA Ops:
  0.0 0.0 copy-start
  0.0 0.9 %broadcast_compare_fusion = pred[8,512]{1,0:T(8,128)(4,1)S(1)} fusion(s32[512]{0:T(512)S(1)} %get-tuple-element.66, s32[8]{0:T(128)} %param.13), kind=kLoop, calls=%fused_computation.18 | loop fusion | flops 4096 | bytes 6176 | tf_op jit(solution)/shard_map/lt | solution.py:49
  0.9 0.8 %copy.9 = s32[8,2]{1,0:T(8,128)S(1)} copy(s32[8,2]{0,1:T(2,128)} %param.12) | data formatting | bytes 128 | tf_op args[4]
  1.6 0.0 copy-start.1
  1.6 0.1 iota_compare_fusion
  1.7 1.1 %and_reduce_fusion = pred[8,2,512]{2,1,0:T(4,128)(4,1)S(1)} fusion(s32[512]{0:T(512)S(1)} %get-tuple-element.65, s32[8,2,16]{2,1,0:T(2,128)} %param.11, pred[8,2,16]{2,1,0:T(4,128)(4,1)S(1)} %iota_compare_fusion), kind=kLoop, calls=%fused_computation.11 | loop fusion | flops 385024 | bytes 11520 | tf_op jit(solution)/shard_map/reduce_or | solution.py:48
  2.8 0.0 copy-done
  2.8 1.6 %fusion.11 = (f32[8,2,16]{2,1,0:T(2,128)S(1)}, f32[8,2,16,512]{3,2,1,0:T(8,128)S(1)}) fusion(bf16[8,2,16,128]{3,2,1,0:T(8,128)(2,1)} %bitcast.31, bf16[8,2,512,128]{3,2,1,0:T(8,128)(2,1)S(1)} %copy-done, pred[8,2,512]{2,1,0:T(4,128)(4,1)S(1)} %broadcast_and_fusion), kind=kOutput, calls=%fused_computation.30 | convolution fusion | flops 33947392 | bytes 2696192 | tf_op jit(solution)/shard_map/bhgd,bhkd->bhgk/dot_general | solution.py:51
  4.4 0.3 fusion.5
  4.7 0.0 copy-done.1
  4.7 1.0 %fusion.4 = f32[8,2,16,128]{3,2,1,0:T(8,128)S(1)} fusion(bf16[8,2,512,128]{3,2,1,0:T(8,128)(2,1)S(1)} %copy-done.1, f32[8,2,16,512]{3,2,1,0:T(8,128)S(1)} %get-tuple-element.64, f32[8,2,16]{2,1,0:T(2,128)S(1)} %broadcast_maximum_fusion), kind=kOutput, calls=%fused_computation.12 | convolution fusion | flops 201457664 | bytes 2753536 | tf_op jit(solution)/shard_map/bhgk,bhkv->bhgv/dot_general | solution.py:58
  5.7 14.8 %all-gather = f32[32,2,16]{2,1,0:T(2,128)S(1)} all-gather(f32[8,2,16]{2,1,0:T(2,128)S(1)} %broadcast_maximum_fusion), channel_id=2, replica_groups=mesh['grp'=2,'seq'=4,'head'=2,'rep'=2] {'seq'}, dimensions={0}, use_global_device_ids=true | all-gather | bytes 5120 | tf_op jit(solution)/shard_map/all_gather | solution.py:14
  20.6 13.1 %all-gather.1 = f32[32,2,16]{2,1,0:T(2,128)S(1)} all-gather(f32[8,2,16]{2,1,0:T(2,128)S(1)} %fusion.5), channel_id=3, replica_groups=mesh['grp'=2,'seq'=4,'head'=2,'rep'=2] {'seq'}, dimensions={0}, use_global_device_ids=true | all-gather | bytes 5120 | tf_op jit(solution)/shard_map/all_gather | solution.py:14
  33.7 15.7 %all-gather.2 = f32[32,2,16,128]{3,2,1,0:T(8,128)S(1)} all-gather(f32[8,2,16,128]{3,2,1,0:T(8,128)S(1)} %fusion.4), channel_id=4, replica_groups=mesh['grp'=2,'seq'=4,'head'=2,'rep'=2] {'seq'}, dimensions={0}, use_global_device_ids=true | all-gather | bytes 655360 | tf_op jit(solution)/shard_map/all_gather | solution.py:14
  49.4 0.7 %while.14 = (s32[]{:T(128)}, f32[8,2,16]{2,1,0:T(2,128)S(1)}, f32[8,2,16]{2,1,0:T(2,128)S(1)}, f32[8,2,16,128]{3,2,1,0:T(8,128)S(1)}, f32[3,8,2,16]{3,2,1,0:T(2,...) while((s32[]{:T(128)}, f32[8,2,16]{2,1,0:T(2,128)S(1)}, ...), condition=%wide.region_4.5_spmd, body=%wide.region_3.4_spmd.sunk | while | flops 99842 | bytes 403557 | solution.py:17
  49.5 0.2 fusion.18
  49.7 0.2 fusion.18
  49.9 0.2 fusion.18
  50.1 0.1 broadcast_divide_fusion
  50.2 0.7 %dynamic-slice_convert_fusion = bf16[8,32,32]{2,1,0:T(8,128)(2,1)} fusion(bf16[8,32,128]{2,1,0:T(8,128)(2,1)S(1)} %bitcast.28, s32[]{:T(128)S(6)} %select_n.18), kind=kLoop, calls=%fused_computation.15 | loop fusion | bytes 32772 | tf_op jit(solution)/shard_map/convert_element_type | solution.py:72
  (12 shorter events, 0.2 us)
Async XLA Ops:
  0.0 2.8 %copy-start = (bf16[8,2,512,128]{3,2,1,0:T(8,128)(2,1)S(1)}, bf16[8,2,512,128]{3,2,1,0:T(8,128)(2,1)}, u32[]{:S(2)}) copy-start(bf16[8,2,512,128]{3,2,1,0:T(8,128)(2,1)} %param.9) | copy-start | bytes 6291460
  1.6 3.0 %copy-start.1 = (bf16[8,2,512,128]{3,2,1,0:T(8,128)(2,1)S(1)}, bf16[8,2,512,128]{3,2,1,0:T(8,128)(2,1)}, u32[]{:S(2)}) copy-start(bf16[8,2,512,128]{3,2,1,0:T(8,128)(2,1)} %param.10) | copy-start | bytes 6291460
where the time goes:
time: 51.2 us; the launch traced here: 50.9 us
  blocking collectives  43.6 us (85%)
  other arithmetic  3.04 us (6%)
  matrix products  2.59 us (5%)
  local copies, waits for them, and re-layouts  1.53 us (3%)
    all_gather x3, blocking collectives, joined(): pieces = jax.tree.map(lambda part: lax.all_gather(part, axis), value)  43.6 us
    dot_general x1, matrix products, local(): jnp.einsum('bhgd,bhkd->bhgk', query_grouped, key_cache, preferred_element...  1.58 us
    reduce_or x1, other arithmetic, local(): picked = jnp.any(matches, axis=2)  1.06 us

commit v1 on v0

v1 whole, which is shorter than its diff:
```python
import functools

import jax
import jax.numpy as jnp
from jax import lax
from jax.experimental import pallas as pl
from jax.experimental.pallas import tpu as pltpu
from jax.sharding import PartitionSpec as P

BLOCK = 64
LOWEST = -1e30
SUB = 8
LANES = 128


def block_transpose(vregs, share):
    n = len(vregs)
    lane_group = lax.broadcasted_iota(jnp.int32, (SUB, LANES), 1) // share
    step = 1
    while step < n:
        low = (lane_group // step) % 2 == 0
        nxt = list(vregs)
        for g in range(n):
            if (g // step) % 2 == 0:
                a, b = vregs[g], vregs[g + step]
                nxt[g] = jnp.where(low, a, pltpu.roll(b, step * share, 1))
                nxt[g + step] = jnp.where(low, pltpu.roll(a, LANES - step * share, 1), b)
        vregs = nxt
        step *= 2
    return vregs


def kernel(n, rows_per_message, q_hbm, k_hbm, v_hbm, idx_hbm, cnt_hbm, len_hbm, out_ref,
           q_ref, k_ref, v_ref, idx_ref, cnt_ref, len_ref, send_buf, recv_buf,
           in_sem, kv_sem, send_sem, recv_sem):
    batch, heads, ctx, width = k_ref.shape
    group = q_ref.shape[1] // heads
    slots = idx_ref.shape[1]
    share = LANES // n
    groups = batch * heads * group // SUB
    chunks = pl.cdiv(groups, n)
    me = lax.axis_index("seq")

    small = [
        pltpu.make_async_copy(src, dst, in_sem.at[i])
        for i, (src, dst) in enumerate(
            ((idx_hbm, idx_ref), (cnt_hbm, cnt_ref), (len_hbm, len_ref), (q_hbm, q_ref))
        )
    ]
    for copy in small:
        copy.start()
    loads = []
    for b in range(batch):
        k_copy = pltpu.make_async_copy(k_hbm.at[b], k_ref.at[b], kv_sem.at[0, b])
        v_copy = pltpu.make_async_copy(v_hbm.at[b], v_ref.at[b], kv_sem.at[1, b])
        k_copy.start()
        v_copy.start()
        loads.append((k_copy, v_copy))

    barrier = pltpu.get_barrier_semaphore()
    for k in range(1, n):
        pl.semaphore_signal(
            barrier, inc=1, device_id={"seq": lax.rem(me + k, n)},
            device_id_type=pl.DeviceIdType.MESH,
        )

    for copy in small:
        copy.wait()

    pairs = batch * heads
    pair = lax.broadcasted_iota(jnp.int32, (pairs, batch), 0)
    row = lax.broadcasted_iota(jnp.int32, (pairs, batch), 1)
    own = pair // heads == row
    length_rows = jnp.broadcast_to(len_ref[...], (pairs, batch)).astype(jnp.float32)
    length = jnp.sum(jnp.where(own, length_rows, 0.0), axis=1, keepdims=True)
    count = jnp.zeros((pairs, 1), jnp.float32)
    for h in range(heads):
        count_rows = jnp.broadcast_to(cnt_ref[h : h + 1, :], (pairs, batch)).astype(jnp.float32)
        count += jnp.sum(
            jnp.where(own & (pair % heads == h), count_rows, 0.0), axis=1, keepdims=True
        )
    slot = lax.broadcasted_iota(jnp.int32, (pairs, slots), 1)
    chosen = jnp.where(slot < count.astype(jnp.int32), idx_ref[...], -1)
    position = me * ctx + lax.broadcasted_iota(jnp.int32, (pairs, ctx), 1)
    block = position // BLOCK
    picked = chosen[:, 0:1] == block
    for s in range(1, slots):
        picked |= chosen[:, s : s + 1] == block
    live = picked & (position < length.astype(jnp.int32))
    bias = jnp.where(live, 0.0, -jnp.inf)

    scale = width ** (-0.5)
    lane = lax.broadcasted_iota(jnp.int32, (SUB, LANES), 1)
    stats = jnp.zeros((SUB, LANES), jnp.float32)
    pending = []
    sends = []
    done = 0
    sent = 0
    message = 0

    def send(first, last, message):
        for k in sorted(range(1, n), key=lambda k: (abs(k - n // 2), -k)):
            peer = lax.rem(me + k, n)
            copy = pltpu.make_async_remote_copy(
                src_ref=send_buf.at[peer, pl.ds(first, last - first)],
                dst_ref=recv_buf.at[k - 1, pl.ds(first, last - first)],
                send_sem=send_sem.at[k - 1, message],
                recv_sem=recv_sem.at[k - 1, message],
                device_id={"seq": peer},
                device_id_type=pl.DeviceIdType.MESH,
            )
            copy.start()
            sends.append(copy)

    for b in range(batch):
        loads[b][0].wait()
        loads[b][1].wait()
        for h in range(heads):
            p_index = b * heads + h
            q = q_ref[b, h * group : (h + 1) * group, :]
            scores = lax.dot_general(
                q, k_ref[b, h], (((1,), (1,)), ((), ())), preferred_element_type=jnp.float32
            )
            scores = scores * scale + bias[p_index : p_index + 1, :]
            top = jnp.maximum(jnp.max(scores, axis=1, keepdims=True), LOWEST)
            weights = jnp.exp(scores - top)
            total = jnp.sum(weights, axis=1, keepdims=True)
            high = weights.astype(jnp.bfloat16)
            rest = (weights - high.astype(jnp.float32)).astype(jnp.bfloat16)
            both = jnp.concatenate([high, rest], axis=0)
            product = jnp.dot(both, v_ref[b, h], preferred_element_type=jnp.float32)
            summed = product[:group] + product[group:]
            for part in range(group // SUB):
                r = p_index * (group // SUB) + part
                c, g = r // n, r % n
                rows = slice(part * SUB, (part + 1) * SUB)
                stats = jnp.where(lane == g * share + c, top[rows], stats)
                stats = jnp.where(lane == g * share + chunks + c, total[rows], stats)
                pending.append(summed[rows])
                if r == groups - 1:
                    pending += [jnp.zeros((SUB, LANES), jnp.float32)] * (n - len(pending))
                if len(pending) == n:
                    for d, packed in enumerate(block_transpose(pending, share)):
                        send_buf[d, c] = packed
                    pending = []
                    done = c + 1
        if b == batch - 1:
            for d in range(n):
                send_buf[d, chunks] = stats
            done = chunks + 1
        if done - sent >= rows_per_message or (b == batch - 1 and done > sent):
            if sent == 0:
                pl.semaphore_wait(barrier, n - 1)
            send(sent, done, message)
            sent = done
            message += 1

    for copy in sends:
        copy.wait_recv()

    sources = [recv_buf.at[k] for k in range(n - 1)]
    held = [stats] + [source[chunks] for source in sources]
    highest = functools.reduce(jnp.maximum, held)
    factors = [jnp.exp(jnp.minimum(h - highest, 0.0)) for h in held]
    totals = [pltpu.roll(h, LANES - chunks, 1) for h in held]
    total = functools.reduce(jnp.add, [f * t for f, t in zip(factors, totals)])
    is_top = lane % share < chunks
    inverse = 1.0 / jnp.where(is_top, total, 1.0)
    factors = [jnp.where(is_top, f * inverse, 0.0) for f in factors]
    base = lane // share * share
    finished = []
    for c in range(chunks):
        result = None
        for i in range(n):
            factor = jnp.take_along_axis(factors[i], base + c, axis=1)
            data = send_buf[me, c] if i == 0 else sources[i - 1][c]
            term = factor * data
            result = term if result is None else result + term
        for g in range(n):
            moved = result if g == 0 else pltpu.roll(result, LANES - g * share, 1)
            finished.append(moved[:, :share])
    per_row = heads * group // SUB
    for b in range(batch):
        out_ref[b] = jnp.concatenate(
            finished[b * per_row : (b + 1) * per_row], axis=0
        ).astype(out_ref.dtype)

    for copy in sends:
        copy.wait_send()


def solution(mesh):
    n = mesh.shape["seq"]

    def local(queries, key_cache, value_cache, indices, counts, lengths):
        batch, heads, ctx, width = key_cache.shape
        value_width = value_cache.shape[3]
        all_heads = queries.shape[1]
        slots = indices.shape[2]
        chunks = pl.cdiv(batch * all_heads // SUB, n)
        rows_per_message = max(1, chunks // 4)
        messages = chunks // rows_per_message + 1
        return pl.pallas_call(
            functools.partial(kernel, n, rows_per_message),
            out_shape=jax.ShapeDtypeStruct(
                (batch, all_heads, value_width // n), jnp.bfloat16
            ),
            in_specs=[pl.BlockSpec(memory_space=pl.ANY)] * 6,
            out_specs=pl.BlockSpec(memory_space=pltpu.VMEM),
            scratch_shapes=[
                pltpu.VMEM(queries.shape, queries.dtype),
                pltpu.VMEM(key_cache.shape, key_cache.dtype),
                pltpu.VMEM(value_cache.shape, value_cache.dtype),
                pltpu.VMEM((batch * heads, slots), jnp.int32),
                pltpu.VMEM((heads, batch), jnp.int32),
                pltpu.VMEM((1, batch), jnp.int32),
                pltpu.VMEM((n, chunks + 1, SUB, LANES), jnp.float32),
                pltpu.VMEM((n - 1, chunks + 1, SUB, LANES), jnp.float32),
                pltpu.SemaphoreType.DMA((4,)),
                pltpu.SemaphoreType.DMA((2, batch)),
                pltpu.SemaphoreType.DMA((n - 1, messages)),
                pltpu.SemaphoreType.DMA((n - 1, messages)),
            ],
            compiler_params=pltpu.CompilerParams(collective_id=0, has_side_effects=True),
        )(
            queries,
            key_cache,
            value_cache,
            indices.reshape(batch * heads, slots),
            counts.T,
            lengths.reshape(1, batch),
        )

    return jax.shard_map(
        local,
        mesh=mesh,
        in_specs=(
            P(("grp", "rep"), "head", None),
            P(("grp", "rep"), "head", "seq", None),
            P(("grp", "rep"), "head", "seq", None),
            P(("grp", "rep"), "head", None),
            P(("grp", "rep"), "head"),
            P(("grp", "rep")),
        ),
        out_specs=P(("grp", "rep"), "head", "seq"),
        check_vma=False,
    )
```

time: 51.2 us -> 18.4 us (0.36)
  blocking collectives: 43.6 us -> 0 us
  Pallas kernels: 0 us -> 16.8 us
  other arithmetic: 3.04 us -> 0 us
  matrix products: 2.59 us -> 0 us
    all_gather x3 -> x0, blocking collectives: 43.6 us -> none  [joined(): pieces = jax.tree.map(lambda part: lax.all_gather(part, axis), value)]
    pallas_call x0 -> x1, Pallas kernels: none -> 16.8 us  [local(): pl.pallas_call(functools.partial(kernel, n, rows_per_message), out_shape=...]
    dot_general x2 -> x0, matrix products: 2.59 us -> none  [the longest x1 1.58 us: local(): jnp.einsum('bhgd,bhkd->bhgk', query_grouped, key_cache, preferred_element...]
    reduce_or x1 -> x0, other arithmetic: 1.06 us -> none  [local(): picked = jnp.any(matches, axis=2)]
    lt x2 -> x0, other arithmetic: 0.95 us -> none  [the longest x1 0.88 us: local(): live = picked & (position[None, None, :] < lengths[:, None, None])]
    convert_element_type x1 -> x0, local copies, waits for them, and re-layouts: 0.72 us -> none  [local(): return result.astype(jnp.bfloat16)]
    unnamed x5 -> x1, local copies, waits for them, and re-layouts: 0.76 us -> 1.47 us
    add x6 -> x0, other arithmetic: 0.62 us -> none  [the longest x3 0.5 us: join_partials(): first_summed * first_factor[..., None]]
where the time goes in v1:
time: 18.4 us; the launch traced here: 18.3 us
  Pallas kernels  16.8 us (91%)
  local copies, waits for them, and re-layouts  1.47 us (8%)
    pallas_call x1, Pallas kernels, local(): pl.pallas_call(functools.partial(kernel, n, rows_per_message), out_shape=...  16.8 us
    unnamed x1, local copies, waits for them, and re-layouts  1.47 us

profile of v1, /device:TPU:0, one launch (start us, length us, event | category | flops | bytes accessed | tf_op | source)
XLA Modules:
  0.0 18.3 jit_solution(8272101450725447497)
XLA Ops:
  0.0 16.8 %shard_map.64 = bf16[8,32,32]{2,1,0:T(8,128)(2,1)} custom-call(bf16[8,32,128]{2,1,0:T(8,128)(2,1)} %q_hbm.1, bf16[8,2,512,128]{3,2,1,0:T(8,128)(2,1)} %k_hbm.1, bf16[8,2,512,128]{3,2,1,0:T(8,128)(2,1)} %v_hbm.1, s32[16,16]{1,0:T(8,128)} %bitcast.3, s32[2,8]{1,0:T(2,128)} %bitcast.4, s32[1,8]{1,0:T(1,128)} %bitcast.5), custom_call_target="tpu_custom_call" | custom-call | tf_op jit(solution)/shard_map/pallas_call | solution.py:203
  16.8 1.5 %copy.8 = bf16[8,32,32]{2,1,0:T(8,128)(2,1)} copy(bf16[8,32,32]{2,1,0:T(8,128)(2,1)} %shard_map.64) | data formatting | bytes 32768

commit v2 on v1

--- a/solution.py
+++ b/solution.py
@@ -10,6 +10,9 @@
 BLOCK = 64
 LOWEST = -1e30
 SUB = 8
+RUN = 4
+LOAD_RUN = 4
+MESSAGES = 2
 LANES = 128
 
 
@@ -30,8 +33,9 @@
     return vregs
 
 
-def kernel(n, rows_per_message, q_hbm, k_hbm, v_hbm, idx_hbm, cnt_hbm, len_hbm, out_ref,
-           q_ref, k_ref, v_ref, idx_ref, cnt_ref, len_ref, send_buf, recv_buf,
+def kernel(n, rows_per_message, run, load_run, q_hbm, k_hbm, v_hbm, idx_hbm, cnt_hbm, len_hbm, out_ref,
+           q_ref, k_ref, v_ref, idx_ref, cnt_ref, len_ref, score_ref, weight_ref,
+           send_buf, recv_buf,
            in_sem, kv_sem, send_sem, recv_sem):
     batch, heads, ctx, width = k_ref.shape
     group = q_ref.shape[1] // heads
@@ -41,28 +45,31 @@
     chunks = pl.cdiv(groups, n)
     me = lax.axis_index("seq")
 
-    small = [
-        pltpu.make_async_copy(src, dst, in_sem.at[i])
-        for i, (src, dst) in enumerate(
-            ((idx_hbm, idx_ref), (cnt_hbm, cnt_ref), (len_hbm, len_ref), (q_hbm, q_ref))
-        )
-    ]
-    for copy in small:
-        copy.start()
-    loads = []
-    for b in range(batch):
-        k_copy = pltpu.make_async_copy(k_hbm.at[b], k_ref.at[b], kv_sem.at[0, b])
-        v_copy = pltpu.make_async_copy(v_hbm.at[b], v_ref.at[b], kv_sem.at[1, b])
-        k_copy.start()
-        v_copy.start()
-        loads.append((k_copy, v_copy))
-
     barrier = pltpu.get_barrier_semaphore()
     for k in range(1, n):
         pl.semaphore_signal(
             barrier, inc=1, device_id={"seq": lax.rem(me + k, n)},
             device_id_type=pl.DeviceIdType.MESH,
         )
+
+    small = [
+        pltpu.make_async_copy(src, dst, in_sem.at[i])
+        for i, (src, dst) in enumerate(
+            ((idx_hbm, idx_ref), (cnt_hbm, cnt_ref), (len_hbm, len_ref), (q_hbm, q_ref))
+        )
+    ]
+    for copy in small:
+        copy.start()
+    loads = [
+        [
+            pltpu.make_async_copy(src.at[b], dst.at[b], kv_sem.at[i, b])
+            for i, (src, dst) in enumerate(((k_hbm, k_ref), (v_hbm, v_ref)))
+        ]
+        for b in range(batch)
+    ]
+    for i in range(2):
+        for load in loads:
+            load[i].start()
 
     for copy in small:
         copy.wait()
@@ -112,31 +119,60 @@
             copy.start()
             sends.append(copy)
 
-    for b in range(batch):
-        loads[b][0].wait()
-        loads[b][1].wait()
+    def score(b):
+        for h in range(heads):
+            scores = lax.dot_general(
+                q_ref[b, h * group : (h + 1) * group, :], k_ref[b, h],
+                (((1,), (1,)), ((), ())), preferred_element_type=jnp.float32,
+            )
+            score_ref[b * heads + h] = scores
+
+    def weigh(b, stats):
         for h in range(heads):
             p_index = b * heads + h
-            q = q_ref[b, h * group : (h + 1) * group, :]
-            scores = lax.dot_general(
-                q, k_ref[b, h], (((1,), (1,)), ((), ())), preferred_element_type=jnp.float32
-            )
-            scores = scores * scale + bias[p_index : p_index + 1, :]
+            scores = score_ref[p_index] * scale + bias[p_index : p_index + 1, :]
             top = jnp.maximum(jnp.max(scores, axis=1, keepdims=True), LOWEST)
             weights = jnp.exp(scores - top)
             total = jnp.sum(weights, axis=1, keepdims=True)
             high = weights.astype(jnp.bfloat16)
             rest = (weights - high.astype(jnp.float32)).astype(jnp.bfloat16)
-            both = jnp.concatenate([high, rest], axis=0)
-            product = jnp.dot(both, v_ref[b, h], preferred_element_type=jnp.float32)
-            summed = product[:group] + product[group:]
+            weight_ref[p_index, :group] = high
+            weight_ref[p_index, group:] = rest
             for part in range(group // SUB):
                 r = p_index * (group // SUB) + part
                 c, g = r // n, r % n
                 rows = slice(part * SUB, (part + 1) * SUB)
                 stats = jnp.where(lane == g * share + c, top[rows], stats)
                 stats = jnp.where(lane == g * share + chunks + c, total[rows], stats)
-                pending.append(summed[rows])
+        return stats
+
+    runs = [range(b, min(b + run, batch)) for b in range(0, batch, run)]
+    for i in range(len(runs) + 1):
+        if i < len(runs):
+            for b in runs[i]:
+                loads[b][0].wait()
+            for b in runs[i]:
+                score(b)
+        if i > 0:
+            for b in runs[i - 1]:
+                stats = weigh(b, stats)
+    for d in range(n):
+        send_buf[d, chunks] = stats
+
+    for b in range(batch):
+        if b % load_run == 0:
+            for later in range(b, min(b + load_run, batch)):
+                loads[later][1].wait()
+        for h in range(heads):
+            p_index = b * heads + h
+            product = jnp.dot(
+                weight_ref[p_index], v_ref[b, h], preferred_element_type=jnp.float32
+            )
+            summed = product[:group] + product[group:]
+            for part in range(group // SUB):
+                r = p_index * (group // SUB) + part
+                c, g = r // n, r % n
+                pending.append(summed[part * SUB : (part + 1) * SUB])
                 if r == groups - 1:
                     pending += [jnp.zeros((SUB, LANES), jnp.float32)] * (n - len(pending))
                 if len(pending) == n:
@@ -145,8 +181,6 @@
                     pending = []
                     done = c + 1
         if b == batch - 1:
-            for d in range(n):
-                send_buf[d, chunks] = stats
             done = chunks + 1
         if done - sent >= rows_per_message or (b == batch - 1 and done > sent):
             if sent == 0:
@@ -198,10 +232,10 @@
         all_heads = queries.shape[1]
         slots = indices.shape[2]
         chunks = pl.cdiv(batch * all_heads // SUB, n)
-        rows_per_message = max(1, chunks // 4)
+        rows_per_message = -(-(chunks + 1) // MESSAGES) if MESSAGES == 1 else max(1, chunks // MESSAGES)
         messages = chunks // rows_per_message + 1
         return pl.pallas_call(
-            functools.partial(kernel, n, rows_per_message),
+            functools.partial(kernel, n, rows_per_message, RUN, LOAD_RUN),
             out_shape=jax.ShapeDtypeStruct(
                 (batch, all_heads, value_width // n), jnp.bfloat16
             ),
@@ -214,6 +248,8 @@
                 pltpu.VMEM((batch * heads, slots), jnp.int32),
                 pltpu.VMEM((heads, batch), jnp.int32),
                 pltpu.VMEM((1, batch), jnp.int32),
+                pltpu.VMEM((batch * heads, all_heads // heads, ctx), jnp.float32),
+                pltpu.VMEM((batch * heads, 2 * all_heads // heads, ctx), jnp.bfloat16),
                 pltpu.VMEM((n, chunks + 1, SUB, LANES), jnp.float32),
                 pltpu.VMEM((n - 1, chunks + 1, SUB, LANES), jnp.float32),
                 pltpu.SemaphoreType.DMA((4,)),
@@ -221,14 +257,19 @@
                 pltpu.SemaphoreType.DMA((n - 1, messages)),
                 pltpu.SemaphoreType.DMA((n - 1, messages)),
             ],
-            compiler_params=pltpu.CompilerParams(collective_id=0, has_side_effects=True),
+            compiler_params=pltpu.CompilerParams(collective_id=0, has_side_effects=True, vmem_limit_bytes=16 << 20),
         )(
-            queries,
-            key_cache,
-            value_cache,
-            indices.reshape(batch * heads, slots),
-            counts.T,
-            lengths.reshape(1, batch),
+            *[
+                pltpu.with_memory_space_constraint(x, pltpu.HBM)
+                for x in (
+                    queries,
+                    key_cache,
+                    value_cache,
+                    indices.reshape(batch * heads, slots),
+                    counts.T,
+                    lengths.reshape(1, batch),
+                )
+            ]
         )
 
     return jax.shard_map(

time: 18.4 us -> 13.2 us (0.72)
  Pallas kernels: 16.8 us -> 12.4 us
  local copies, waits for them, and re-layouts: 1.47 us -> 0.63 us
    pallas_call x1, Pallas kernels: 16.8 us -> 12.4 us  [local(): pl.pallas_call(functools.partial(kernel, n, rows_per_message, RUN, LOAD_R...]
    unnamed x1, local copies, waits for them, and re-layouts: 1.47 us -> 0.63 us
where the time goes in v2:
time: 13.2 us; the launch traced here: 13.1 us
  Pallas kernels  12.4 us (94%)
  local copies, waits for them, and re-layouts  0.63 us (5%)
    pallas_call x1, Pallas kernels, local(): pl.pallas_call(functools.partial(kernel, n, rows_per_message, RUN, LOAD_R...  12.4 us
    unnamed x1, local copies, waits for them, and re-layouts  0.63 us

profile of v2, /device:TPU:0, one launch (start us, length us, event | category | flops | bytes accessed | tf_op | source)
XLA Modules:
  0.0 13.1 jit_solution(3940865895534351906)
XLA Ops:
  0.0 12.4 %shard_map.64 = bf16[8,32,32]{2,1,0:T(8,128)(2,1)S(1)} custom-call(bf16[8,32,128]{2,1,0:T(8,128)(2,1)} %q_hbm.1, bf16[8,2,512,128]{3,2,1,0:T(8,128)(2,1)} %k_hbm.1, bf16[8,2,512,128]{3,2,1,0:T(8,128)(2,1)} %v_hbm.1, s32[16,16]{1,0:T(8,128)} %bitcast.3, s32[2,8]{1,0:T(2,128)} %bitcast.4, s32[1,8]{1,0:T(1,128)} %bitcast.5), custom_call_target="tpu_custom_call" | custom-call | tf_op jit(solution)/shard_map/pallas_call | solution.py:237
  12.4 0.6 %copy.8 = bf16[8,32,32]{2,1,0:T(8,128)(2,1)} copy(bf16[8,32,32]{2,1,0:T(8,128)(2,1)S(1)} %shard_map.64) | data formatting | bytes 32768

commit v3 on v2

--- a/solution.py
+++ b/solution.py
@@ -12,7 +12,7 @@
 SUB = 8
 RUN = 4
 LOAD_RUN = 4
-MESSAGES = 2
+MESSAGES = 1
 LANES = 128
 
 
@@ -101,23 +101,36 @@
     stats = jnp.zeros((SUB, LANES), jnp.float32)
     pending = []
     sends = []
+    parts = []
     done = 0
     sent = 0
     message = 0
 
+    def exchange(first, last, message, source, peer):
+        return pltpu.make_async_remote_copy(
+            src_ref=send_buf.at[peer, pl.ds(first, last - first)],
+            dst_ref=recv_buf.at[source, pl.ds(first, last - first)],
+            send_sem=send_sem.at[peer, message],
+            recv_sem=recv_sem.at[source, message],
+            device_id={"seq": peer},
+            device_id_type=pl.DeviceIdType.MESH,
+        )
+
+    upper = 2 * me // n
+    peers = []
+    for k in range(n - 1):
+        down = n - 1 - k
+        down = down - 1 + (down - me + n - 1) // n
+        up = k + 1 - (me - k + n - 1) // n
+        peers.append(upper * up + (1 - upper) * down)
+    others = [lax.rem(me + k, n) for k in range(1, n)]
+
     def send(first, last, message):
-        for k in sorted(range(1, n), key=lambda k: (abs(k - n // 2), -k)):
-            peer = lax.rem(me + k, n)
-            copy = pltpu.make_async_remote_copy(
-                src_ref=send_buf.at[peer, pl.ds(first, last - first)],
-                dst_ref=recv_buf.at[k - 1, pl.ds(first, last - first)],
-                send_sem=send_sem.at[k - 1, message],
-                recv_sem=recv_sem.at[k - 1, message],
-                device_id={"seq": peer},
-                device_id_type=pl.DeviceIdType.MESH,
-            )
+        for peer in peers:
+            copy = exchange(first, last, message, me, peer)
             copy.start()
             sends.append(copy)
+        parts.append((first, last, message))
 
     def score(b):
         for h in range(heads):
@@ -157,7 +170,7 @@
             for b in runs[i - 1]:
                 stats = weigh(b, stats)
     for d in range(n):
-        send_buf[d, chunks] = stats
+        send_buf[d, 0] = stats
 
     for b in range(batch):
         if b % load_run == 0:
@@ -177,11 +190,9 @@
                     pending += [jnp.zeros((SUB, LANES), jnp.float32)] * (n - len(pending))
                 if len(pending) == n:
                     for d, packed in enumerate(block_transpose(pending, share)):
-                        send_buf[d, c] = packed
+                        send_buf[d, c + 1] = packed
                     pending = []
-                    done = c + 1
-        if b == batch - 1:
-            done = chunks + 1
+                    done = c + 2
         if done - sent >= rows_per_message or (b == batch - 1 and done > sent):
             if sent == 0:
                 pl.semaphore_wait(barrier, n - 1)
@@ -189,30 +200,32 @@
             sent = done
             message += 1
 
-    for copy in sends:
-        copy.wait_recv()
-
-    sources = [recv_buf.at[k] for k in range(n - 1)]
-    held = [stats] + [source[chunks] for source in sources]
-    highest = functools.reduce(jnp.maximum, held)
-    factors = [jnp.exp(jnp.minimum(h - highest, 0.0)) for h in held]
-    totals = [pltpu.roll(h, LANES - chunks, 1) for h in held]
-    total = functools.reduce(jnp.add, [f * t for f, t in zip(factors, totals)])
+    base = lane // share * share
     is_top = lane % share < chunks
-    inverse = 1.0 / jnp.where(is_top, total, 1.0)
-    factors = [jnp.where(is_top, f * inverse, 0.0) for f in factors]
-    base = lane // share * share
     finished = []
-    for c in range(chunks):
-        result = None
-        for i in range(n):
-            factor = jnp.take_along_axis(factors[i], base + c, axis=1)
-            data = send_buf[me, c] if i == 0 else sources[i - 1][c]
-            term = factor * data
-            result = term if result is None else result + term
-        for g in range(n):
-            moved = result if g == 0 else pltpu.roll(result, LANES - g * share, 1)
-            finished.append(moved[:, :share])
+    factors = None
+    for first, last, message in parts:
+        for source in others:
+            exchange(first, last, message, source, me).wait_recv()
+        if factors is None:
+            held = [stats] + [recv_buf[source, 0] for source in others]
+            highest = functools.reduce(jnp.maximum, held)
+            factors = [jnp.exp(jnp.minimum(h - highest, 0.0)) for h in held]
+            totals = [pltpu.roll(h, LANES - chunks, 1) for h in held]
+            total = functools.reduce(jnp.add, [f * t for f, t in zip(factors, totals)])
+            inverse = 1.0 / jnp.where(is_top, total, 1.0)
+            factors = [jnp.where(is_top, f * inverse, 0.0) for f in factors]
+            factors = [
+                [jnp.take_along_axis(f, base + c, axis=1) for f in factors]
+                for c in range(chunks)
+            ]
+        for c in range(max(first, 1) - 1, last - 1):
+            result = factors[c][0] * send_buf[me, c + 1]
+            for i, source in enumerate(others):
+                result += factors[c][i + 1] * recv_buf[source, c + 1]
+            for g in range(n):
+                moved = result if g == 0 else pltpu.roll(result, LANES - g * share, 1)
+                finished.append(moved[:, :share])
     per_row = heads * group // SUB
     for b in range(batch):
         out_ref[b] = jnp.concatenate(
@@ -251,11 +264,11 @@
                 pltpu.VMEM((batch * heads, all_heads // heads, ctx), jnp.float32),
                 pltpu.VMEM((batch * heads, 2 * all_heads // heads, ctx), jnp.bfloat16),
                 pltpu.VMEM((n, chunks + 1, SUB, LANES), jnp.float32),
-                pltpu.VMEM((n - 1, chunks + 1, SUB, LANES), jnp.float32),
+                pltpu.VMEM((n, chunks + 1, SUB, LANES), jnp.float32),
                 pltpu.SemaphoreType.DMA((4,)),
                 pltpu.SemaphoreType.DMA((2, batch)),
-                pltpu.SemaphoreType.DMA((n - 1, messages)),
-                pltpu.SemaphoreType.DMA((n - 1, messages)),
+                pltpu.SemaphoreType.DMA((n, messages)),
+                pltpu.SemaphoreType.DMA((n, messages)),
             ],
             compiler_params=pltpu.CompilerParams(collective_id=0, has_side_effects=True, vmem_limit_bytes=16 << 20),
         )(

time: 13.2 us -> 12.7 us (0.962)
  Pallas kernels: 12.4 us -> 12 us
    pallas_call x1, Pallas kernels: 12.4 us -> 12 us  [local(): pl.pallas_call(functools.partial(kernel, n, rows_per_message, RUN, LOAD_R...]
where the time goes in v3:
time: 12.7 us; the launch traced here: 12.6 us
  Pallas kernels  12 us (94%)
  local copies, waits for them, and re-layouts  0.63 us (5%)
    pallas_call x1, Pallas kernels, local(): pl.pallas_call(functools.partial(kernel, n, rows_per_message, RUN, LOAD_R...  12 us
    unnamed x1, local copies, waits for them, and re-layouts  0.63 us

profile of v3, /device:TPU:0, one launch (start us, length us, event | category | flops | bytes accessed | tf_op | source)
XLA Modules:
  0.0 12.6 jit_solution(8421044334337015804)
XLA Ops:
  0.0 12.0 %shard_map.64 = bf16[8,32,32]{2,1,0:T(8,128)(2,1)S(1)} custom-call(bf16[8,32,128]{2,1,0:T(8,128)(2,1)} %q_hbm.1, bf16[8,2,512,128]{3,2,1,0:T(8,128)(2,1)} %k_hbm.1, bf16[8,2,512,128]{3,2,1,0:T(8,128)(2,1)} %v_hbm.1, s32[16,16]{1,0:T(8,128)} %bitcast.3, s32[2,8]{1,0:T(2,128)} %bitcast.4, s32[1,8]{1,0:T(1,128)} %bitcast.5), custom_call_target="tpu_custom_call" | custom-call | tf_op jit(solution)/shard_map/pallas_call | solution.py:250
  12.0 0.6 %copy.8 = bf16[8,32,32]{2,1,0:T(8,128)(2,1)} copy(bf16[8,32,32]{2,1,0:T(8,128)(2,1)S(1)} %shard_map.64) | data formatting | bytes 32768
